TPU v7x, 32 devices: a whole 2x2x4 slice. The times are simulated.
32 devices in a mesh: dp: 8 (over y, x, core), tensor: 4 (over z).
Axes of the slice: x: 2, y: 2, z: 4, core: 2. Of those that a mesh axis runs over, the one named last changes fastest.
Arguments:
- node_features: bfloat16 [8192, 768], P(('dp', 'tensor')), may hold values from -6 to 6
- graph_ids: int32 [64, 128], P('dp'), may hold values from 0 to 5, never falling along the last dimension, each value on 1 to 32 neighbouring positions
- degree: int32 [8192], P(('dp', 'tensor')), may hold values from 0 to 511
- distance: int32 [8192, 128], P('dp'), may hold values from 0 to 511
- out_grad: bfloat16 [8192, 768], P(('dp', 'tensor')), may hold values from -6 to 6
- qkv_weight: bfloat16 [3, 768, 768], P(None, 'tensor'), may hold values from -0.21875 to 0.21875
- qv_bias: float32 [2, 768], P(None, 'tensor'), may hold values from -3 to 3
- out_weight: bfloat16 [768, 768], P('tensor'), may hold values from -0.625 to 0.625
- out_bias: float32 [768], replicated, may hold values from -3 to 3
- norm1_gain: float32 [768], replicated, may hold values from 0.5 to 1.5
- norm1_shift: float32 [768], replicated, may hold values from -2 to 2
- ffn_in_weight: bfloat16 [768, 768], P('tensor'), may hold values from -0.21875 to 0.21875
- ffn_in_bias: float32 [768], P('tensor'), may hold values from -3 to 3
- ffn_out_weight: bfloat16 [768, 768], P('tensor'), may hold values from -0.21875 to 0.21875
- ffn_out_bias: float32 [768], replicated, may hold values from -3 to 3
- norm2_gain: float32 [768], replicated, may hold values from 0.5 to 1.5
- norm2_shift: float32 [768], replicated, may hold values from -2 to 2
- degree_table: bfloat16 [512, 768], replicated, may hold values from -3 to 3
- spatial_table: bfloat16 [32, 512], P('tensor'), may hold values from -4 to 4
Outputs:
- layer_out: bfloat16 [8192, 768], P(('dp', 'tensor'))
- input_grad: bfloat16 [8192, 768], P(('dp', 'tensor'))
- qkv_weight_grad: float32 [3, 768, 768], P(None, 'tensor')
- qv_bias_grad: float32 [2, 768], P(None, 'tensor')
- out_weight_grad: float32 [768, 768], P('tensor')
- out_bias_grad: float32 [768], replicated
- norm1_gain_grad: float32 [768], replicated
- norm1_shift_grad: float32 [768], replicated
- ffn_in_weight_grad: float32 [768, 768], P('tensor')
- ffn_in_bias_grad: float32 [768], P('tensor')
- ffn_out_weight_grad: float32 [768, 768], P('tensor')
- ffn_out_bias_grad: float32 [768], replicated
- norm2_gain_grad: float32 [768], replicated
- norm2_shift_grad: float32 [768], replicated
- degree_table_grad: float32 [512, 768], replicated
- spatial_table_grad: float32 [32, 512], P('tensor')
Inputs may be any that keep to these rules, and one draw needn't show every extreme that they name: `graph_ids`: graph numbers never fall along a packed block; a graph holds at most a quarter of 128 nodes, and in every block some graph holds exactly that many.
All inputs are finite; a program needn't handle non-finite values.
Results may differ from a plain program's by a relative error of at most 0.018.
Values may be sent and summed in bfloat16 or wider, within the bound.
A program may use at most 128 MiB of HBM per device.

v0:
```python
import math
import jax
import jax.numpy as jnp
from jax import lax
from jax.sharding import PartitionSpec as P

norm_eps = 1e-05
masked_score = -1e30


def norm_rows(hidden_rows, gain, shift):
    row_mean = jnp.mean(hidden_rows, axis=1, keepdims=True)
    centered = hidden_rows - row_mean
    variance = jnp.mean(centered * centered, axis=1, keepdims=True)
    inverse = lax.rsqrt(variance + norm_eps)
    normed = centered * inverse
    return (normed, inverse, (normed * gain + shift).astype(jnp.bfloat16))


def norm_back(upstream, normed, inverse, gain):
    scaled = upstream * gain
    first_mean = jnp.mean(scaled, axis=1, keepdims=True)
    second_mean = jnp.mean(scaled * normed, axis=1, keepdims=True)
    through = inverse * (scaled - first_mean - normed * second_mean)
    return (through, jnp.sum(upstream * normed, axis=0), jnp.sum(upstream, axis=0))


def whole_rows(part_rows):
    return lax.all_gather(part_rows, "tensor", axis=0, tiled=True)


def whole_grads(part_rows):
    return lax.all_gather(part_rows, "tensor", axis=0, tiled=True)


def branch_sum(partial_rows):
    return lax.psum_scatter(
        partial_rows.astype(jnp.bfloat16), "tensor", scatter_dimension=0, tiled=True
    ).astype(jnp.float32)


def feature_grad_sum(partial_rows):
    return lax.psum_scatter(
        partial_rows.astype(jnp.bfloat16), "tensor", scatter_dimension=0, tiled=True
    ).astype(jnp.float32)


def inner_rows(left, right):
    return lax.dot_general(
        left, right, (((0,), (0,)), ((), ())), preferred_element_type=jnp.float32
    )


def against_cols(left, right):
    return lax.dot_general(
        left, right, (((1,), (1,)), ((), ())), preferred_element_type=jnp.float32
    )


def distance_onehot(distance_block, table_rows):
    flat_index = distance_block.reshape(1, -1)
    return (
        lax.broadcasted_iota(jnp.int32, (table_rows, flat_index.shape[1]), 0) == flat_index
    ).astype(jnp.bfloat16)


def pair_bias_block(distance_block, table_heads):
    onehot = distance_onehot(distance_block, table_heads.shape[1])
    looked = jnp.dot(table_heads, onehot, preferred_element_type=jnp.float32)
    return looked.astype(jnp.bfloat16).reshape(
        table_heads.shape[0], distance_block.shape[0], distance_block.shape[1]
    )


def split_heads(matrix, block_count, head_count):
    return matrix.reshape(block_count, -1, head_count, matrix.shape[1] // head_count)


def scores_of(query_heads, key_heads, bias, graph_rows, score_scale):
    raw_scores = jnp.einsum(
        "bihd,bjhd->bhij", query_heads, key_heads, preferred_element_type=jnp.float32
    ) * score_scale + bias.astype(jnp.float32)
    same_graph = (graph_rows[:, :, None] == graph_rows[:, None, :])[:, None]
    return jnp.where(same_graph, raw_scores, masked_score)


def attend_forward(inputs, score_scale):
    query, keys, values, bias, graph_rows = inputs
    block_count = graph_rows.shape[0]
    head_count = bias.shape[1]
    query_heads = split_heads(query, block_count, head_count)
    key_heads = split_heads(keys, block_count, head_count)
    value_heads = split_heads(values, block_count, head_count)
    scores = scores_of(query_heads, key_heads, bias, graph_rows, score_scale)
    row_max = jnp.max(scores, axis=-1, keepdims=True)
    shifted = jnp.exp(scores - row_max)
    row_total = jnp.sum(shifted, axis=-1, keepdims=True)
    probs_low = (shifted / row_total).astype(jnp.bfloat16)
    mixed = jnp.einsum(
        "bhij,bjhd->bihd", probs_low, value_heads, preferred_element_type=jnp.float32
    )
    return (mixed.reshape(query.shape).astype(jnp.bfloat16), (row_max + jnp.log(row_total))[..., 0])


def attend_back(inputs, score_scale):
    query, keys, values, mixed_grad, bias, graph_rows, log_total = inputs
    block_count = graph_rows.shape[0]
    head_count = bias.shape[1]
    query_heads = split_heads(query, block_count, head_count)
    key_heads = split_heads(keys, block_count, head_count)
    value_heads = split_heads(values, block_count, head_count)
    grad_heads = split_heads(mixed_grad, block_count, head_count)
    scores = scores_of(query_heads, key_heads, bias, graph_rows, score_scale)
    probs = jnp.exp(scores - log_total[..., None])
    probs_low = probs.astype(jnp.bfloat16)
    values_grad = jnp.einsum(
        "bhij,bihd->bjhd", probs_low, grad_heads, preferred_element_type=jnp.float32
    )
    probs_grad = jnp.einsum(
        "bihd,bjhd->bhij", grad_heads, value_heads, preferred_element_type=jnp.float32
    )
    scores_grad = (
        probs * (probs_grad - jnp.sum(probs * probs_grad, axis=-1, keepdims=True))
    ).astype(jnp.bfloat16)
    query_grad = (
        jnp.einsum("bhij,bjhd->bihd", scores_grad, key_heads, preferred_element_type=jnp.float32)
        * score_scale
    )
    keys_grad = (
        jnp.einsum("bhij,bihd->bjhd", scores_grad, query_heads, preferred_element_type=jnp.float32)
        * score_scale
    )
    stacked = jnp.stack(
        [
            query_grad.reshape(query.shape),
            keys_grad.reshape(query.shape),
            values_grad.reshape(query.shape),
        ],
        axis=1,
    ).astype(jnp.bfloat16)
    return (stacked, scores_grad)


def shards(
    node_features,
    graph_ids,
    degree,
    distance,
    out_grad,
    qkv_weight,
    qv_bias,
    out_weight,
    out_bias,
    norm1_gain,
    norm1_shift,
    ffn_in_weight,
    ffn_in_bias,
    ffn_out_weight,
    ffn_out_bias,
    norm2_gain,
    norm2_shift,
    degree_table,
    spatial_table,
):
    block_count, block_size = graph_ids.shape
    row_count = block_count * block_size
    local_width = qkv_weight.shape[1]
    model_width = qkv_weight.shape[2]
    head_count = spatial_table.shape[0]
    table_rows = spatial_table.shape[1]
    score_scale = 1.0 / math.sqrt(local_width // head_count)
    group_blocks = 4
    group_count = block_count // group_blocks

    def grouped(array):
        return array.reshape((group_count, -1) + array.shape[1:])

    degree_onehot = (
        degree[:, None] == lax.broadcasted_iota(jnp.int32, (1, degree_table.shape[0]), 1)
    ).astype(jnp.bfloat16)
    embedded = node_features.astype(jnp.float32) + jnp.dot(
        degree_onehot, degree_table, preferred_element_type=jnp.float32
    )
    normed1, inverse1, act1 = norm_rows(embedded, norm1_gain, norm1_shift)
    whole1 = whole_rows(act1)
    qkv_flat = qkv_weight.reshape(3 * local_width, model_width)
    projected = against_cols(whole1, qkv_flat).reshape(row_count, 3, local_width)
    query = (projected[:, 0] + qv_bias[0]).astype(jnp.bfloat16)
    keys = projected[:, 1].astype(jnp.bfloat16)
    values = (projected[:, 2] + qv_bias[1]).astype(jnp.bfloat16)
    distance_blocks = distance.reshape(block_count, block_size, block_size)
    pair_bias = lax.map(
        lambda distance_block: pair_bias_block(distance_block, spatial_table), distance_blocks
    )
    mixed_groups, log_totals = lax.map(
        lambda inputs: attend_forward(inputs, score_scale),
        (grouped(query), grouped(keys), grouped(values), grouped(pair_bias), grouped(graph_ids)),
    )
    mixed = mixed_groups.reshape(row_count, local_width)
    attended = branch_sum(jnp.dot(mixed, out_weight, preferred_element_type=jnp.float32)) + out_bias
    residual1 = embedded + attended
    normed2, inverse2, act2 = norm_rows(residual1, norm2_gain, norm2_shift)
    upstream = out_grad.astype(jnp.float32)
    ffn_out_bias_grad = jnp.sum(upstream, axis=0)
    whole2 = whole_rows(act2)
    pre_act = against_cols(whole2, ffn_in_weight) + ffn_in_bias
    hidden = jax.nn.gelu(pre_act, approximate=False).astype(jnp.bfloat16)
    ffn_branch = branch_sum(jnp.dot(hidden, ffn_out_weight, preferred_element_type=jnp.float32))
    layer_out = (residual1 + ffn_branch + ffn_out_bias).astype(jnp.bfloat16)
    grad_whole = whole_grads(out_grad)
    ffn_out_grad = inner_rows(hidden, grad_whole)
    hidden_grad = against_cols(grad_whole, ffn_out_weight)
    unused_value, gelu_pull = jax.vjp(
        lambda pre_value: jax.nn.gelu(pre_value, approximate=False), pre_act
    )
    pre_grad = gelu_pull(hidden_grad)[0].astype(jnp.bfloat16)
    ffn_in_bias_grad = jnp.sum(pre_grad.astype(jnp.float32), axis=0)
    ffn_in_grad = inner_rows(pre_grad, whole2)
    normed2_grad = feature_grad_sum(
        jnp.dot(pre_grad, ffn_in_weight, preferred_element_type=jnp.float32)
    )
    through2, norm2_gain_grad, norm2_shift_grad = norm_back(
        normed2_grad, normed2, inverse2, norm2_gain
    )
    residual1_grad = upstream + through2
    out_bias_grad = jnp.sum(residual1_grad, axis=0)
    attn_whole = whole_grads(residual1_grad.astype(jnp.bfloat16))
    out_weight_grad = inner_rows(mixed, attn_whole)
    mixed_grad = against_cols(attn_whole, out_weight).astype(jnp.bfloat16)
    stacked_groups, scores_grads = lax.map(
        lambda inputs: attend_back(inputs, score_scale),
        (
            grouped(query),
            grouped(keys),
            grouped(values),
            grouped(mixed_grad),
            grouped(pair_bias),
            grouped(graph_ids),
            log_totals,
        ),
    )
    stacked = stacked_groups.reshape(row_count, 3, local_width)
    stacked_float = stacked.astype(jnp.float32)
    qv_bias_grad = jnp.stack(
        [jnp.sum(stacked_float[:, 0], axis=0), jnp.sum(stacked_float[:, 2], axis=0)]
    )
    stacked_flat = stacked.reshape(row_count, 3 * local_width)
    qkv_weight_grad = inner_rows(stacked_flat, whole1).reshape(3, local_width, model_width)
    normed1_grad = feature_grad_sum(
        jnp.dot(stacked_flat, qkv_flat, preferred_element_type=jnp.float32)
    )

    def table_step(running, block_pair):
        distance_block, grad_block = block_pair
        onehot = distance_onehot(distance_block, table_rows)
        return (running + against_cols(grad_block.reshape(head_count, -1), onehot), None)

    spatial_grad, unused_carry = lax.scan(
        table_step,
        jnp.zeros((head_count, table_rows), jnp.float32),
        (distance_blocks, scores_grads.reshape(block_count, head_count, block_size, block_size)),
    )
    through1, norm1_gain_grad, norm1_shift_grad = norm_back(
        normed1_grad, normed1, inverse1, norm1_gain
    )
    embedded_grad = residual1_grad + through1
    input_grad = embedded_grad.astype(jnp.bfloat16)
    grad_upper = embedded_grad.astype(jnp.bfloat16)
    grad_lower = (embedded_grad - grad_upper.astype(jnp.float32)).astype(jnp.bfloat16)
    degree_grad = inner_rows(degree_onehot, grad_upper) + inner_rows(degree_onehot, grad_lower)
    (
        ffn_in_grad,
        ffn_in_bias_grad,
        ffn_out_grad,
        qkv_weight_grad,
        qv_bias_grad,
        out_weight_grad,
        spatial_grad,
    ) = lax.psum(
        (
            ffn_in_grad,
            ffn_in_bias_grad,
            ffn_out_grad,
            qkv_weight_grad,
            qv_bias_grad,
            out_weight_grad,
            spatial_grad,
        ),
        "dp",
    )
    (
        degree_grad,
        out_bias_grad,
        ffn_out_bias_grad,
        norm1_gain_grad,
        norm1_shift_grad,
        norm2_gain_grad,
        norm2_shift_grad,
    ) = lax.psum(
        (
            degree_grad,
            out_bias_grad,
            ffn_out_bias_grad,
            norm1_gain_grad,
            norm1_shift_grad,
            norm2_gain_grad,
            norm2_shift_grad,
        ),
        ("dp", "tensor"),
    )
    return (
        layer_out,
        input_grad,
        qkv_weight_grad,
        qv_bias_grad,
        out_weight_grad,
        out_bias_grad,
        norm1_gain_grad,
        norm1_shift_grad,
        ffn_in_grad,
        ffn_in_bias_grad,
        ffn_out_grad,
        ffn_out_bias_grad,
        norm2_gain_grad,
        norm2_shift_grad,
        degree_grad,
        spatial_grad,
    )


def solution(mesh):
    return jax.shard_map(
        shards,
        mesh=mesh,
        in_specs=(
            P(("dp", "tensor"), None),
            P("dp", None),
            P(("dp", "tensor")),
            P("dp", None),
            P(("dp", "tensor"), None),
            P(None, "tensor", None),
            P(None, "tensor"),
            P("tensor", None),
            P(),
            P(),
            P(),
            P("tensor", None),
            P("tensor"),
            P("tensor", None),
            P(),
            P(),
            P(),
            P(),
            P("tensor", None),
        ),
        out_specs=(
            P(("dp", "tensor"), None),
            P(("dp", "tensor"), None),
            P(None, "tensor", None),
            P(None, "tensor"),
            P("tensor", None),
            P(),
            P(),
            P(),
            P("tensor", None),
            P("tensor"),
            P("tensor", None),
            P(),
            P(),
            P(),
            P(),
            P("tensor", None),
        ),
        check_vma=False,
    )
```

profile of v0, /device:TPU:0, one launch (start us, length us, event | category | flops | bytes accessed | tf_op | source)
XLA Modules:
  0.0 616.1 jit_solution(1584065396677808624)
XLA Ops:
  10.4 54.4 %while.45 = (s32[]{:T(128)}, bf16[8,8,128,128]{2,3,1,0:T(8,128)(2,1)}, s32[8,128,128]{2,1,0:T(8,128)}, bf16[8,512]{1,0:T(8,128)(2,1)S(1)}, s32[]{:T(128)}) while((s32[]{:T(128)}, bf16[8,8,128,128]{2,3,1,0:T(8,128)(2,1)}, s32[8,128,128]{2,1,0:T(8,128)}, bf16[8,512]{1,0:T(8,128)(2,1)S(1)}, s32[]{:T(128)}) %tuple.145), condition=%wide.region_3.4_spmd, body=%wide.region_2.3_spmd.sunk | while | flops 142737408 | bytes 1515597 | solution.py:192
  11.3 5.0 fusion.125
  18.1 5.0 fusion.125
  24.9 5.0 fusion.125
  31.7 5.0 fusion.125
  38.5 5.0 fusion.125
  45.3 5.0 fusion.125
  52.1 5.0 fusion.125
  58.8 5.0 fusion.125
  64.8 2.5 fusion.35
  71.2 2.7 squeeze.31
  74.0 2.3 fusion.53
  76.3 10.7 %while.46 = (s32[]{:T(128)}, bf16[2,512,192]{1,2,0:T(8,128)(2,1)S(1)}, f32[2,4,8,128]{3,2,1,0:T(8,128)S(1)}, bf16[2,512,192]{1,2,0:T(8,128)(2,1)}, s32[2,4,128]{...) while((s32[]{:T(128)}, ...), condition=%wide.region_7.8_spmd, body=%wide.region_4.7_spmd.sunk | while | flops 55734272 | bytes 11933821 | solution.py:195
  83.8 1.9 fusion.127
  87.0 2.9 convolution_convert_fusion.5
  90.0 38.2 %reduce-scatter.5.cloned.1.call-done = bf16[256,768]{1,0:T(8,128)(2,1)} async-done(((bf16[1024,768]{1,0:T(8,128)(2,1)}), bf16[256,768]{1,0:T(8,128)(2,1)}) %reduce-scatter.5.cloned.1.call-update) | async-done | bytes 393232 | tf_op jit(solution)/shard_map/reduce_scatter | solution.py:37
  131.2 10.5 %reduce-scatter.9.cloned.1.call-start = ((), (), s32[]{:S(2)}) async-start(), calls=%async_computation.9 | async-start | bytes 1966080 | tf_op jit(solution)/shard_map/reduce_scatter | solution.py:43
  141.7 25.0 %all-gather.7.cloned.1.call-done = bf16[1024,768]{1,0:T(8,128)(2,1)} async-done(((bf16[256,768]{1,0:T(8,128)(2,1)}), bf16[1024,768]{1,0:T(8,128)(2,1)}) %all-gather.7.cloned.1.call-update) | async-done | bytes 1572880 | tf_op jit(solution)/shard_map/all_gather | solution.py:29
  166.7 2.1 convolution_add_fusion.1
  168.8 35.3 %all-gather.9.cloned.1.call-done = bf16[1024,768]{1,0:T(8,128)(2,1)} async-done(((bf16[256,768]{1,0:T(8,128)(2,1)}), bf16[1024,768]{1,0:T(8,128)(2,1)}) %all-gather.9.cloned.1.call-update) | async-done | bytes 1572880 | tf_op jit(solution)/shard_map/all_gather | solution.py:33
  204.0 4.6 convert_reduce_fusion.3
  211.8 2.9 convolution_convert_fusion.4
  214.7 30.2 %reduce-scatter.9.cloned.1.call-done = bf16[256,768]{1,0:T(8,128)(2,1)} async-done(((bf16[1024,768]{1,0:T(8,128)(2,1)}), bf16[256,768]{1,0:T(8,128)(2,1)}) %reduce-scatter.9.cloned.1.call-update) | async-done | bytes 393232 | tf_op jit(solution)/shard_map/reduce_scatter | solution.py:43
  246.4 35.6 %reduce-scatter.7.cloned.1.call-done = bf16[256,768]{1,0:T(8,128)(2,1)} async-done(((bf16[1024,768]{1,0:T(8,128)(2,1)}), bf16[256,768]{1,0:T(8,128)(2,1)}) %reduce-scatter.7.cloned.1.call-update) | async-done | bytes 393232 | tf_op jit(solution)/shard_map/reduce_scatter | solution.py:37
  282.0 2.4 fusion.64
  285.3 35.9 %all-gather.11.cloned.1.call-done = bf16[1024,768]{1,0:T(8,128)(2,1)} async-done(((bf16[256,768]{1,0:T(8,128)(2,1)}), bf16[1024,768]{1,0:T(8,128)(2,1)}) %all-gather.11.cloned.1.call-update) | async-done | bytes 1572880 | tf_op jit(solution)/shard_map/all_gather | solution.py:33
  321.3 2.1 convolution_convert_fusion.6
  324.1 21.3 %while.47 = (s32[]{:T(128)}, bf16[2,512,3,192]{1,3,2,0:T(8,128)(2,1)}, bf16[2,4,8,128,128]{4,3,2,1,0:T(8,128)(2,1)}, bf16[2,512,192]{1,2,0:T(8,128)(2,1)S(1)}, s...) while((s32[]{:T(128)}, ...), condition=%wide.region_17.18_spmd, body=%wide.region_15.17_spmd.sunk | while | flops 133918720 | bytes 29841552 | solution.py:230
  327.0 2.2 multiply_reduce_fusion.4
  337.6 2.2 multiply_reduce_fusion.4
  345.4 2.5 copy.98
  349.2 2.6 convolution_convert_fusion.2
  353.2 2.4 fusion.74
  358.2 2.3 fusion.33
  360.8 25.4 %reduce-scatter.11.cloned.1.call-done = bf16[256,768]{1,0:T(8,128)(2,1)} async-done(((bf16[1024,768]{1,0:T(8,128)(2,1)}), bf16[256,768]{1,0:T(8,128)(2,1)}) %reduce-scatter.11.cloned.1.call-update) | async-done | bytes 393232 | tf_op jit(solution)/shard_map/reduce_scatter | solution.py:43
  391.3 58.4 %while.48 = (s32[]{:T(128)}, f32[8,512]{1,0:T(8,128)S(1)}, bf16[8,8,128,128]{3,2,1,0:T(8,128)(2,1)}, s32[8,128,128]{2,1,0:T(8,128)}, s32[]{:T(128)}, /*index=5*/s32[]{:T(128)}) while((s32[]{:T(128)}, f32[8,512]{1,0:T(8,128)S(1)}, bf16[8,8,128,128]{3,2,1,0:T(8,128)(2,1)}, s32[8,128,128]{2,1,0:T(8,128)}, s32[]{:T(128)}, ...), condition=%wide.region_44.45_spmd.clone, body=%wide.region_43.44_spmd.clone.sunk | while | flops 142614528 | bytes 1015903 | solution.py:258
  393.3 5.5 fusion.144
  400.5 5.5 fusion.144
  407.8 5.5 fusion.144
  415.1 5.5 fusion.144
  422.4 5.5 fusion.144
  429.7 5.5 fusion.144
  437.0 5.5 fusion.144
  444.3 5.5 fusion.144
  450.6 24.9 %all-reduce.1 = (f32[2,192]{1,0:T(2,128)}, f32[192]{0:T(256)}, f32[8,512]{1,0:T(8,128)}) all-reduce(f32[2,192]{1,0:T(2,128)S(1)} %pad_maximum_fusion, f32[192]{0:T(256)S(1)} %get-tuple-element.308, f32[8,512]{1,0:T(8,128)S(1)} %get-tuple-element.161), channel_id=1, replica_groups=mesh['dp'=8,'tensor'=4] {'dp'}, use_global_device_ids=true, to_apply=%region_24.25 | all-reduce | flops 4672 | bytes 37376 | tf_op jit(solution)/shard_map/psum | solution.py:279
  475.5 39.5 %all-reduce = (f32[768]{0:T(1024)}, f32[768]{0:T(1024)}, f32[768]{0:T(1024)}, f32[768]{0:T(1024)}, f32[768]{0:T(1024)}, /*index=5*/f32[768]{0:T(1024)}) all-reduce(f32[768]{0:T(1024)S(1)} %get-tuple-element.306, f32[768]{0:T(1024)S(1)} %get-tuple-element.235, ...), channel_id=1, replica_groups=mesh['dp'=8,'tensor'=4] {'dp','tensor'}, use_global_device_ids=true, to_apply=%region_27.28 | all-reduce | flops 4608 | bytes 36864 | tf_op jit(solution)/shard_map/psum | solution.py:299
  515.0 87.4 %all-reduce.6.cloned.1.call-done = f32[512,768]{1,0:T(8,128)} async-done(((f32[512,768]{1,0:T(8,128)}), f32[512,768]{1,0:T(8,128)}) %all-reduce.6.cloned.1.call-update) | async-done | bytes 1572880 | tf_op jit(solution)/shard_map/psum | solution.py:299
  602.4 2.9 copy.228
  (255 shorter events, 85.5 us)
Async XLA Ops:
  7.2 57.7 %copy-start = (bf16[3,192,768]{2,1,0:T(8,128)(2,1)S(1)}, bf16[3,192,768]{2,1,0:T(8,128)(2,1)}, u32[]{:S(2)}) copy-start(bf16[3,192,768]{2,1,0:T(8,128)(2,1)} %param.32) | copy-start | bytes 2654212
  7.2 2.1 copy-start.27
  7.2 2.1 copy-start.29
  7.2 3.2 copy-start.36
  7.2 57.6 %all-gather.5.cloned.1.call-start = ((), (), s32[]{:S(2)}) async-start(), calls=%async_computation.4 | async-start | bytes 1966080 | tf_op jit(solution)/shard_map/all_gather | solution.py:29
  9.1 119.2 %copy-start.1 = (f32[256,768]{1,0:T(8,128)}, f32[256,768]{1,0:T(8,128)S(1)}, u32[]{:S(2)}) copy-start(f32[256,768]{1,0:T(8,128)S(1)} %get-tuple-element.332) | copy-start | bytes 2359300
  10.3 117.9 %reduce-scatter.5.cloned.1.call-start = ((), (), s32[]{:S(2)}) async-start(), calls=%async_computation.5 | async-start | bytes 1966080 | tf_op jit(solution)/shard_map/reduce_scatter | solution.py:37
  10.4 54.4 %copy-start.33 = (f32[2,192]{1,0:T(2,128)S(1)}, f32[2,192]{1,0:T(2,128)}, u32[]{:S(2)}) copy-start(f32[2,192]{1,0:T(2,128)} %param.33) | copy-start | bytes 4612
  71.2 5.1 copy-start.23
  71.2 5.1 copy-start.25
  87.0 3.0 copy-start.8
  87.0 41.3 %copy-start.30 = (f32[768]{0:T(1024)S(1)}, f32[768]{0:T(1024)}, u32[]{:S(2)}) copy-start(f32[768]{0:T(1024)} %param.35) | copy-start | bytes 9220
  89.9 39.8 %copy-start.26 = (f32[768]{0:T(1024)S(1)}, f32[768]{0:T(1024)}, u32[]{:S(2)}) copy-start(f32[768]{0:T(1024)} %param.42) | copy-start | bytes 9220
  89.9 39.8 %copy-start.31 = (f32[768]{0:T(1024)S(1)}, f32[768]{0:T(1024)}, u32[]{:S(2)}) copy-start(f32[768]{0:T(1024)} %param.43) | copy-start | bytes 9220
  89.9 76.8 %copy-start.16 = (bf16[192,768]{1,0:T(8,128)(2,1)S(1)}, bf16[192,768]{1,0:T(8,128)(2,1)}, u32[]{:S(2)}) copy-start(bf16[192,768]{1,0:T(8,128)(2,1)} %param.38) | copy-start | bytes 884740
  89.9 76.8 %copy-start.34 = (f32[192]{0:T(256)S(1)}, f32[192]{0:T(256)}, u32[]{:S(2)}) copy-start(f32[192]{0:T(256)} %param.39) | copy-start | bytes 2308
  89.9 76.8 %all-gather.7.cloned.1.call-start = ((), (), s32[]{:S(2)}) async-start(), calls=%async_computation.6 | async-start | bytes 1966080 | tf_op jit(solution)/shard_map/all_gather | solution.py:29
  130.7 73.4 %all-gather.9.cloned.1.call-start = ((), (), s32[]{:S(2)}) async-start(), calls=%async_computation.8 | async-start | bytes 1966080 | tf_op jit(solution)/shard_map/all_gather | solution.py:33
  131.2 113.7 %reduce-scatter.9.cloned.1.call-start = ((), (), s32[]{:S(2)}) async-start(), calls=%async_computation.9 | async-start | bytes 1966080 | tf_op jit(solution)/shard_map/reduce_scatter | solution.py:43
  204.0 4.6 copy-start.17
  208.7 1.9 copy-start.15
  210.4 71.5 %reduce-scatter.7.cloned.1.call-start = ((), (), s32[]{:S(2)}) async-start(), calls=%async_computation.7 | async-start | bytes 1966080 | tf_op jit(solution)/shard_map/reduce_scatter | solution.py:37
  211.8 34.6 %copy-start.10 = (bf16[1024,192]{0,1:T(8,128)(2,1)}, bf16[1024,192]{0,1:T(8,128)(2,1)S(1)}, u32[]{:S(2)}) copy-start(bf16[1024,192]{0,1:T(8,128)(2,1)S(1)} %multiply_convert_fusion.1) | copy-start | bytes 1179652
  211.8 70.2 %copy-start.32 = (f32[768]{0:T(1024)S(1)}, f32[768]{0:T(1024)}, u32[]{:S(2)}) copy-start(f32[768]{0:T(1024)} %param.41) | copy-start | bytes 9220
  214.7 106.6 %all-gather.11.cloned.1.call-start = ((), (), s32[]{:S(2)}) async-start(), calls=%async_computation.10 | async-start | bytes 1966080 | tf_op jit(solution)/shard_map/all_gather | solution.py:33
  246.4 74.9 %copy-start.24 = (bf16[192,768]{1,0:T(8,128)(2,1)S(1)}, bf16[192,768]{1,0:T(8,128)(2,1)}, u32[]{:S(2)}) copy-start(bf16[192,768]{1,0:T(8,128)(2,1)} %param.34) | copy-start | bytes 884740
  284.4 39.7 %copy-start.3 = (f32[256,768]{1,0:T(8,128)}, f32[256,768]{1,0:T(8,128)S(1)}, u32[]{:S(2)}) copy-start(f32[256,768]{1,0:T(8,128)S(1)} %get-tuple-element.307) | copy-start | bytes 2359300
  285.2 101.0 %reduce-scatter.11.cloned.1.call-start = ((), (), s32[]{:S(2)}) async-start(), calls=%async_computation.11 | async-start | bytes 1966080 | tf_op jit(solution)/shard_map/reduce_scatter | solution.py:43
  348.2 1.0 copy-start.18
  351.8 1.4 copy-start.5
  351.8 3.9 copy-start.11
  351.8 5.1 copy-start.9
  351.8 163.2 %all-reduce.8.cloned.1.call-start = ((), (), s32[]{:S(2)}) async-start(), calls=%async_computation.13 | async-start | bytes 7077888 | tf_op jit(solution)/shard_map/psum | solution.py:279
  353.2 2.4 copy-start.12
  353.2 3.8 copy-start.13
  355.6 2.6 copy-start.19
  355.6 2.6 copy-start.35
  360.5 25.7 %copy-start.2 = (f32[256,768]{1,0:T(8,128)S(1)}, f32[256,768]{1,0:T(8,128)}, u32[]{:S(2)}) copy-start(f32[256,768]{1,0:T(8,128)} %copy-done.1) | copy-start | bytes 2359300
  360.5 27.1 %copy-start.4 = (f32[256,768]{1,0:T(8,128)S(1)}, f32[256,768]{1,0:T(8,128)}, u32[]{:S(2)}) copy-start(f32[256,768]{1,0:T(8,128)} %copy-done.3) | copy-start | bytes 2359300
  360.6 241.8 %all-reduce.6.cloned.1.call-start = ((), (), s32[]{:S(2)}) async-start(), calls=%async_computation.12 | async-start | bytes 3145728 | tf_op jit(solution)/shard_map/psum | solution.py:299
  360.8 28.2 %copy-start.28 = (s32[256]{0:T(256)S(1)}, s32[256]{0:T(256)}, u32[]{:S(2)}) copy-start(s32[256]{0:T(256)} %param.29) | copy-start | bytes 3076
  389.0 2.3 copy-start.7
  391.3 58.4 %copy-start.6 = (bf16[2,512,3,192]{1,3,2,0:T(8,128)(2,1)S(1)}, bf16[2,512,3,192]{1,3,2,0:T(8,128)(2,1)}, u32[]{:S(2)}) copy-start(bf16[2,512,3,192]{1,3,2,0:T(8,128)(2,1)} %get-tuple-element.159) | copy-start | bytes 3538948
  515.0 90.3 %copy-start.22 = (f32[192,768]{1,0:T(8,128)S(1)}, f32[192,768]{1,0:T(8,128)}, u32[]{:S(2)}) copy-start(f32[192,768]{1,0:T(8,128)} %get-tuple-element.612) | copy-start | bytes 1769476
  602.4 3.7 copy-start.21
  602.4 4.5 copy-start.20
  605.3 2.5 copy-start.14
Sparse Core Ops, SparseCore 0:
  10.4 39.8 all-gather.4
  90.0 38.1 reduce-scatter.4
  130.8 35.8 all-gather.6
  168.1 35.8 all-gather.8
  210.6 34.2 reduce-scatter.8
  247.6 34.2 reduce-scatter.6
  285.4 35.8 all-gather.10
  351.9 34.2 reduce-scatter.10
  391.0 72.7 all-reduce.7
  469.6 132.7 all-reduce.5
where the time goes:
time: 627 us; the launch traced here: 616 us
  waiting for transfers between devices  314 us (50%)
  matrix products  130 us (21%)
  blocking collectives  64.4 us (10%)
  local copies, waits for them, and re-layouts  62.3 us (10%)
  other arithmetic  19 us (3%)
  between operations  15 us (2%)
  starting transfers between devices  11 us (2%)
    psum x1, waiting for transfers between devices, shards(): lax.psum((degree_grad, out_bias_grad, ffn_out_bias_grad, norm1_gain_grad,...  87.4 us
    reduce_scatter x2, waiting for transfers between devices, branch_sum(): lax.psum_scatter(partial_rows.astype(jnp.bfloat16), 'tensor', scatter_dim...  73.8 us
    all_gather x2, waiting for transfers between devices, whole_grads(): return lax.all_gather(part_rows, 'tensor', axis=0, tiled=True)  71.2 us
    reduce_scatter x2, waiting for transfers between devices, feature_grad_sum(): lax.psum_scatter(partial_rows.astype(jnp.bfloat16), 'tensor', scatter_dim...  55.6 us
    dot_general x12, matrix products, against_cols(): lax.dot_general(left, right, (((1,), (1,)), ((), ())), preferred_element_...  55.1 us
    dot_general x8, matrix products, pair_bias_block(): looked = jnp.dot(table_heads, onehot, preferred_element_type=jnp.float32)  40 us
    psum x1, blocking collectives, shards(): lax.psum((degree_grad, out_bias_grad, ffn_out_bias_grad, norm1_gain_grad,...  39.5 us
    all_gather x2, waiting for transfers between devices, whole_rows(): return lax.all_gather(part_rows, 'tensor', axis=0, tiled=True)  25 us
  transfers between devices with their start and end apart: 10, of which 8 were waited for; matrix products, arithmetic and copies ran while one was open for 22% of the time, Pallas kernels for 0%

commit v1 on v0

--- a/solution.py
+++ b/solution.py
@@ -6,6 +6,22 @@
 
 norm_eps = 1e-05
 masked_score = -1e30
+
+
+def gather_around(x, axis, dim):
+    ways, here, step = (lax.axis_size(axis), lax.axis_index(axis), x.shape[dim])
+    dims = [n * ways if d == dim else n for d, n in enumerate(x.shape)]
+    full = lax.dynamic_update_slice_in_dim(jnp.zeros(dims, x.dtype), x, here * step, axis=dim)
+    going_up = going_down = x
+    for far in range(1, ways // 2 + 1):
+        going_up = lax.ppermute(going_up, axis, [(d, (d + 1) % ways) for d in range(ways)])
+        full = lax.dynamic_update_slice_in_dim(full, going_up, (here - far) % ways * step, axis=dim)
+        if 2 * far < ways:
+            going_down = lax.ppermute(going_down, axis, [(d, (d - 1) % ways) for d in range(ways)])
+            full = lax.dynamic_update_slice_in_dim(
+                full, going_down, (here + far) % ways * step, axis=dim
+            )
+    return full
 
 
 def norm_rows(hidden_rows, gain, shift):
@@ -30,7 +46,7 @@
 
 
 def whole_grads(part_rows):
-    return lax.all_gather(part_rows, "tensor", axis=0, tiled=True)
+    return gather_around(part_rows, "tensor", 0)
 
 
 def branch_sum(partial_rows):

time: 627 us -> 604 us (0.963)
  waiting for transfers between devices: 314 us -> 265 us
  starting transfers between devices: 11 us -> 26.7 us
  local copies, waits for them, and re-layouts: 62.3 us -> 70 us
    all_gather x2 -> x0, waiting for transfers between devices: 71.2 us -> none  [whole_grads(): return lax.all_gather(part_rows, 'tensor', axis=0, tiled=True)]
    ppermute x0 -> x6, waiting for transfers between devices: none -> 46.7 us  [the longest x4 40.5 us: gather_around(): lax.ppermute(going_up, axis, [(d, (d + 1) % ways) for d in range(ways)])]
    ppermute x0 -> x6, starting transfers between devices: none -> 26.2 us  [the longest x4 18.8 us: gather_around(): lax.ppermute(going_up, axis, [(d, (d + 1) % ways) for d in range(ways)])]
    all_gather x2, waiting for transfers between devices: 25 us -> 3.68 us  [whole_rows(): return lax.all_gather(part_rows, 'tensor', axis=0, tiled=True)]
    reduce_scatter x2, starting transfers between devices: 10.5 us -> 0.08 us  [feature_grad_sum(): lax.psum_scatter(partial_rows.astype(jnp.bfloat16), 'tensor', scatter_dim...]
    dynamic_update_slice x0 -> x7, local copies, waits for them, and re-layouts: none -> 6.39 us  [the longest x4 4.08 us: gather_around(): lax.dynamic_update_slice_in_dim(full, going_up, (here - far) % ways * ste...]
  transfers between devices with their start and end apart: 10 -> 14, of which waited for: 8 -> 12; matrix products, arithmetic and copies ran while one was open for 22% -> 24% of each run, Pallas kernels for 0% -> 0%
where the time goes in v1:
time: 604 us; the launch traced here: 593 us
  waiting for transfers between devices  265 us (44%)
  matrix products  132 us (22%)
  local copies, waits for them, and re-layouts  70 us (12%)
  blocking collectives  64.4 us (11%)
  starting transfers between devices  26.7 us (4%)
  other arithmetic  19 us (3%)
  between operations  15 us (2%)
    psum x1, waiting for transfers between devices, shards(): lax.psum((degree_grad, out_bias_grad, ffn_out_bias_grad, norm1_gain_grad,...  87.6 us
    reduce_scatter x2, waiting for transfers between devices, branch_sum(): lax.psum_scatter(partial_rows.astype(jnp.bfloat16), 'tensor', scatter_dim...  73.3 us
    dot_general x12, matrix products, against_cols(): lax.dot_general(left, right, (((1,), (1,)), ((), ())), preferred_element_...  55.1 us
    reduce_scatter x2, waiting for transfers between devices, feature_grad_sum(): lax.psum_scatter(partial_rows.astype(jnp.bfloat16), 'tensor', scatter_dim...  54 us
    ppermute x4, waiting for transfers between devices, gather_around(): lax.ppermute(going_up, axis, [(d, (d + 1) % ways) for d in range(ways)])  40.5 us
    dot_general x8, matrix products, pair_bias_block(): looked = jnp.dot(table_heads, onehot, preferred_element_type=jnp.float32)  40 us
    psum x1, blocking collectives, shards(): lax.psum((degree_grad, out_bias_grad, ffn_out_bias_grad, norm1_gain_grad,...  39.5 us
    psum x1, blocking collectives, shards(): lax.psum((ffn_in_grad, ffn_in_bias_grad, ffn_out_grad, qkv_weight_grad, q...  24.9 us
  transfers between devices with their start and end apart: 14, of which 12 were waited for; matrix products, arithmetic and copies ran while one was open for 24% of the time, Pallas kernels for 0%

profile of v1, /device:TPU:0, one launch (start us, length us, event | category | flops | bytes accessed | tf_op | source)
XLA Modules:
  0.0 593.0 jit_solution(8676907522961289133)
XLA Ops:
  10.4 54.4 %while.45 = (s32[]{:T(128)}, bf16[8,8,128,128]{2,3,1,0:T(8,128)(2,1)}, s32[8,128,128]{2,1,0:T(8,128)}, bf16[8,512]{1,0:T(8,128)(2,1)S(1)}, s32[]{:T(128)}) while((s32[]{:T(128)}, bf16[8,8,128,128]{2,3,1,0:T(8,128)(2,1)}, s32[8,128,128]{2,1,0:T(8,128)}, bf16[8,512]{1,0:T(8,128)(2,1)S(1)}, s32[]{:T(128)}) %tuple.143), condition=%wide.region_3.4_spmd, body=%wide.region_2.3_spmd.sunk | while | flops 142737408 | bytes 1515597 | solution.py:208
  11.3 5.0 fusion.125
  18.1 5.0 fusion.125
  24.9 5.0 fusion.125
  31.7 5.0 fusion.125
  38.5 5.0 fusion.125
  45.3 5.0 fusion.125
  52.1 5.0 fusion.125
  58.9 5.0 fusion.125
  64.9 2.5 fusion.35
  71.2 2.7 squeeze.31
  76.3 10.6 %while.46 = (s32[]{:T(128)}, bf16[2,512,192]{1,2,0:T(8,128)(2,1)S(1)}, f32[2,4,8,128]{3,2,1,0:T(8,128)S(1)}, bf16[2,512,192]{1,2,0:T(8,128)(2,1)}, s32[2,4,128]{...) while((s32[]{:T(128)}, ...), condition=%wide.region_7.8_spmd, body=%wide.region_4.7_spmd.sunk | while | flops 55734272 | bytes 11933821 | solution.py:211
  87.0 2.9 convolution_convert_fusion.5
  90.0 38.2 %reduce-scatter.5.cloned.1.call-done = bf16[256,768]{1,0:T(8,128)(2,1)} async-done(((bf16[1024,768]{1,0:T(8,128)(2,1)}), bf16[256,768]{1,0:T(8,128)(2,1)}) %reduce-scatter.5.cloned.1.call-update) | async-done | bytes 393232 | tf_op jit(solution)/shard_map/reduce_scatter | solution.py:53
  130.9 3.7 collective-permute-start.1
  134.6 12.7 %collective-permute-done = bf16[256,768]{1,0:T(8,128)(2,1)S(1)} collective-permute-done((bf16[256,768]{1,0:T(8,128)(2,1)S(1)}, bf16[256,768]{1,0:T(8,128)(2,1)S(1)}, u32[]{:S(2)}, u32[]{:S(2)}) %collective-permute-start) | collective-permute-done | bytes 393248 | tf_op jit(solution)/shard_map/ppermute | solution.py:17
  147.3 14.7 %collective-permute-start.2 = (bf16[256,768]{1,0:T(8,128)(2,1)S(1)}, bf16[256,768]{1,0:T(8,128)(2,1)}, u32[]{:S(2)}, u32[]{:S(2)}) collective-permute-start(bf16[256,768]{1,0:T(8,128)(2,1)S(1)} %collective-permute-done), channel_id=1, source_target_pairs={{0,1},{1,2},{2,3},{3,0},{4,5},{5,6},{6,7},{7,4},{8,9},{9,10},{10,1... | collective-permute-start | bytes 1179656 | tf_op jit(solution)/shard_map/ppermute | solution.py:17
  164.7 5.6 collective-permute-done.1
  171.1 8.5 %collective-permute-done.2 = bf16[256,768]{1,0:T(8,128)(2,1)} collective-permute-done((bf16[256,768]{1,0:T(8,128)(2,1)S(1)}, bf16[256,768]{1,0:T(8,128)(2,1)}, u32[]{:S(2)}, u32[]{:S(2)}) %collective-permute-start.2) | collective-permute-done | bytes 393248 | tf_op jit(solution)/shard_map/ppermute | solution.py:17
  181.4 3.7 all-gather.5.cloned.1.call-done
  187.1 4.6 convert_reduce_fusion.3
  194.9 2.9 convolution_convert_fusion.4
  197.9 30.6 %reduce-scatter.9.cloned.1.call-done = bf16[256,768]{1,0:T(8,128)(2,1)} async-done(((bf16[1024,768]{1,0:T(8,128)(2,1)}), bf16[256,768]{1,0:T(8,128)(2,1)}) %reduce-scatter.9.cloned.1.call-update) | async-done | bytes 393232 | tf_op jit(solution)/shard_map/reduce_scatter | solution.py:59
  230.0 35.0 %reduce-scatter.7.cloned.1.call-done = bf16[256,768]{1,0:T(8,128)(2,1)} async-done(((bf16[1024,768]{1,0:T(8,128)(2,1)}), bf16[256,768]{1,0:T(8,128)(2,1)}) %reduce-scatter.7.cloned.1.call-update) | async-done | bytes 393232 | tf_op jit(solution)/shard_map/reduce_scatter | solution.py:53
  265.0 2.4 fusion.64
  269.7 3.7 collective-permute-start.4
  273.4 10.0 %collective-permute-done.3 = bf16[256,768]{1,0:T(8,128)(2,1)S(1)} collective-permute-done((bf16[256,768]{1,0:T(8,128)(2,1)S(1)}, bf16[256,768]{1,0:T(8,128)(2,1)S(1)}, u32[]{:S(2)}, u32[]{:S(2)}) %collective-permute-start.3) | collective-permute-done | bytes 393248 | tf_op jit(solution)/shard_map/ppermute | solution.py:17
  283.4 3.8 collective-permute-start.5
  289.4 9.3 %collective-permute-done.5 = bf16[256,768]{1,0:T(8,128)(2,1)S(1)} collective-permute-done((bf16[256,768]{1,0:T(8,128)(2,1)S(1)}, bf16[256,768]{1,0:T(8,128)(2,1)S(1)}, u32[]{:S(2)}, u32[]{:S(2)}) %collective-permute-start.5) | collective-permute-done | bytes 393248 | tf_op jit(solution)/shard_map/ppermute | solution.py:17
  301.6 21.2 %while.47 = (s32[]{:T(128)}, bf16[2,512,3,192]{1,3,2,0:T(8,128)(2,1)}, bf16[2,4,8,128,128]{4,3,2,1,0:T(8,128)(2,1)}, bf16[2,512,192]{1,2,0:T(8,128)(2,1)S(1)}, s...) while((s32[]{:T(128)}, ...), condition=%wide.region_17.18_spmd, body=%wide.region_15.17_spmd.sunk | while | flops 133918720 | bytes 32987336 | solution.py:246
  322.8 2.5 copy.98
  326.6 2.6 convolution_convert_fusion.2
  330.2 2.7 fusion.75
  334.2 2.8 fusion.73
  339.6 23.4 %reduce-scatter.11.cloned.1.call-done = bf16[256,768]{1,0:T(8,128)(2,1)} async-done(((bf16[1024,768]{1,0:T(8,128)(2,1)}), bf16[256,768]{1,0:T(8,128)(2,1)}) %reduce-scatter.11.cloned.1.call-update) | async-done | bytes 393232 | tf_op jit(solution)/shard_map/reduce_scatter | solution.py:59
  368.1 58.4 %while.48 = (s32[]{:T(128)}, f32[8,512]{1,0:T(8,128)S(1)}, bf16[8,8,128,128]{3,2,1,0:T(8,128)(2,1)}, s32[8,128,128]{2,1,0:T(8,128)}, s32[]{:T(128)}, /*index=5*/s32[]{:T(128)}) while((s32[]{:T(128)}, f32[8,512]{1,0:T(8,128)S(1)}, bf16[8,8,128,128]{3,2,1,0:T(8,128)(2,1)}, s32[8,128,128]{2,1,0:T(8,128)}, s32[]{:T(128)}, ...), condition=%wide.region_44.45_spmd.clone, body=%wide.region_43.44_spmd.clone.sunk | while | flops 142614528 | bytes 1015903 | solution.py:274
  370.0 5.5 fusion.144
  377.3 5.5 fusion.144
  384.6 5.5 fusion.144
  391.9 5.5 fusion.144
  399.2 5.5 fusion.144
  406.4 5.5 fusion.144
  413.7 5.5 fusion.144
  421.0 5.5 fusion.144
  427.3 24.9 %all-reduce.1 = (f32[2,192]{1,0:T(2,128)}, f32[192]{0:T(256)}, f32[8,512]{1,0:T(8,128)}) all-reduce(f32[2,192]{1,0:T(2,128)S(1)} %pad_maximum_fusion, f32[192]{0:T(256)S(1)} %get-tuple-element.308, f32[8,512]{1,0:T(8,128)S(1)} %get-tuple-element.161), channel_id=1, replica_groups=mesh['dp'=8,'tensor'=4] {'dp'}, use_global_device_ids=true, to_apply=%region_24.25 | all-reduce | flops 4672 | bytes 37376 | tf_op jit(solution)/shard_map/psum | solution.py:295
  452.2 39.5 %all-reduce = (f32[768]{0:T(1024)}, f32[768]{0:T(1024)}, f32[768]{0:T(1024)}, f32[768]{0:T(1024)}, f32[768]{0:T(1024)}, /*index=5*/f32[768]{0:T(1024)}) all-reduce(f32[768]{0:T(1024)S(1)} %get-tuple-element.306, f32[768]{0:T(1024)S(1)} %get-tuple-element.235, ...), channel_id=1, replica_groups=mesh['dp'=8,'tensor'=4] {'dp','tensor'}, use_global_device_ids=true, to_apply=%region_27.28 | all-reduce | flops 4608 | bytes 36864 | tf_op jit(solution)/shard_map/psum | solution.py:315
  491.7 87.6 %all-reduce.6.cloned.1.call-done = f32[512,768]{1,0:T(8,128)} async-done(((f32[512,768]{1,0:T(8,128)}), f32[512,768]{1,0:T(8,128)}) %all-reduce.6.cloned.1.call-update) | async-done | bytes 1572880 | tf_op jit(solution)/shard_map/psum | solution.py:315
  579.3 2.9 copy.236
  (276 shorter events, 107.3 us)
Async XLA Ops:
  7.2 57.7 %copy-start = (bf16[3,192,768]{2,1,0:T(8,128)(2,1)S(1)}, bf16[3,192,768]{2,1,0:T(8,128)(2,1)}, u32[]{:S(2)}) copy-start(bf16[3,192,768]{2,1,0:T(8,128)(2,1)} %param.32) | copy-start | bytes 2654212
  7.2 2.1 copy-start.28
  7.2 2.1 copy-start.30
  7.2 57.6 %all-gather.3.cloned.1.call-start = ((), (), s32[]{:S(2)}) async-start(), calls=%async_computation.4 | async-start | bytes 1966080 | tf_op jit(solution)/shard_map/all_gather | solution.py:45
  9.1 119.2 %copy-start.1 = (f32[256,768]{1,0:T(8,128)}, f32[256,768]{1,0:T(8,128)S(1)}, u32[]{:S(2)}) copy-start(f32[256,768]{1,0:T(8,128)S(1)} %get-tuple-element.334) | copy-start | bytes 2359300
  9.1 1.3 copy-start.37
  10.3 117.9 %reduce-scatter.5.cloned.1.call-start = ((), (), s32[]{:S(2)}) async-start(), calls=%async_computation.5 | async-start | bytes 1966080 | tf_op jit(solution)/shard_map/reduce_scatter | solution.py:53
  10.4 54.4 %copy-start.34 = (f32[2,192]{1,0:T(2,128)S(1)}, f32[2,192]{1,0:T(2,128)}, u32[]{:S(2)}) copy-start(f32[2,192]{1,0:T(2,128)} %param.33) | copy-start | bytes 4612
  73.9 2.4 copy-start.24
  73.9 2.4 copy-start.26
  87.0 2.9 copy-start.10
  87.0 41.2 %copy-start.31 = (f32[768]{0:T(1024)S(1)}, f32[768]{0:T(1024)}, u32[]{:S(2)}) copy-start(f32[768]{0:T(1024)} %param.35) | copy-start | bytes 9220
  89.9 39.8 %copy-start.27 = (f32[768]{0:T(1024)S(1)}, f32[768]{0:T(1024)}, u32[]{:S(2)}) copy-start(f32[768]{0:T(1024)} %param.42) | copy-start | bytes 9220
  89.9 39.8 %copy-start.32 = (f32[768]{0:T(1024)S(1)}, f32[768]{0:T(1024)}, u32[]{:S(2)}) copy-start(f32[768]{0:T(1024)} %param.43) | copy-start | bytes 9220
  89.9 95.1 %all-gather.5.cloned.1.call-start = ((), (), s32[]{:S(2)}) async-start(), calls=%async_computation.6 | async-start | bytes 1966080 | tf_op jit(solution)/shard_map/all_gather | solution.py:45
  130.7 97.9 %reduce-scatter.9.cloned.1.call-start = ((), (), s32[]{:S(2)}) async-start(), calls=%async_computation.8 | async-start | bytes 1966080 | tf_op jit(solution)/shard_map/reduce_scatter | solution.py:59
  130.7 16.6 %collective-permute-start = (bf16[256,768]{1,0:T(8,128)(2,1)S(1)}, bf16[256,768]{1,0:T(8,128)(2,1)S(1)}, u32[]{:S(2)}, u32[]{:S(2)}) collective-permute-start(bf16[256,768]{1,0:T(8,128)(2,1)S(1)} %copy-done.15), channel_id=1, source_target_pairs={{0,1},{1,2},{2,3},{3,0},{4,5},{5,6},{6,7},{7,4},{8,9},{9,10},{10,1... | collective-permute-start | bytes 1179656 | tf_op jit(solution)/shard_map/ppermute | solution.py:17
  130.9 39.4 %collective-permute-start.1 = (bf16[256,768]{1,0:T(8,128)(2,1)S(1)}, bf16[256,768]{1,0:T(8,128)(2,1)S(1)}, u32[]{:S(2)}, u32[]{:S(2)}) collective-permute-start(bf16[256,768]{1,0:T(8,128)(2,1)S(1)} %copy-done.15), channel_id=1, source_target_pairs={{0,3},{1,0},{2,1},{3,2},{4,7},{5,4},{6,5},{7,6},{8,11},{9,8},{10,9... | collective-permute-start | bytes 1179656 | tf_op jit(solution)/shard_map/ppermute | solution.py:20
  147.3 32.3 %collective-permute-start.2 = (bf16[256,768]{1,0:T(8,128)(2,1)S(1)}, bf16[256,768]{1,0:T(8,128)(2,1)}, u32[]{:S(2)}, u32[]{:S(2)}) collective-permute-start(bf16[256,768]{1,0:T(8,128)(2,1)S(1)} %collective-permute-done), channel_id=1, source_target_pairs={{0,1},{1,2},{2,3},{3,0},{4,5},{5,6},{6,7},{7,4},{8,9},{9,10},{10,1... | collective-permute-start | bytes 1179656 | tf_op jit(solution)/shard_map/ppermute | solution.py:17
  163.2 21.8 %copy-start.35 = (f32[192]{0:T(256)S(1)}, f32[192]{0:T(256)}, u32[]{:S(2)}) copy-start(f32[192]{0:T(256)} %param.39) | copy-start | bytes 2308
  187.1 4.7 copy-start.18
  191.8 1.8 copy-start.16
  193.6 71.4 %reduce-scatter.7.cloned.1.call-start = ((), (), s32[]{:S(2)}) async-start(), calls=%async_computation.7 | async-start | bytes 1966080 | tf_op jit(solution)/shard_map/reduce_scatter | solution.py:53
  194.9 3.0 copy-start.12
  197.8 67.2 %copy-start.33 = (f32[768]{0:T(1024)S(1)}, f32[768]{0:T(1024)}, u32[]{:S(2)}) copy-start(f32[768]{0:T(1024)} %param.41) | copy-start | bytes 9220
  197.9 165.1 %reduce-scatter.11.cloned.1.call-start = ((), (), s32[]{:S(2)}) async-start(), calls=%async_computation.9 | async-start | bytes 1966080 | tf_op jit(solution)/shard_map/reduce_scatter | solution.py:59
  267.4 2.1 copy-start.3
  269.6 29.9 %copy-start.25 = (bf16[192,768]{1,0:T(8,128)(2,1)S(1)}, bf16[192,768]{1,0:T(8,128)(2,1)}, u32[]{:S(2)}) copy-start(bf16[192,768]{1,0:T(8,128)(2,1)} %param.34) | copy-start | bytes 884740
  269.6 13.8 %collective-permute-start.3 = (bf16[256,768]{1,0:T(8,128)(2,1)S(1)}, bf16[256,768]{1,0:T(8,128)(2,1)S(1)}, u32[]{:S(2)}, u32[]{:S(2)}) collective-permute-start(bf16[256,768]{1,0:T(8,128)(2,1)S(1)} %get-tuple-element.314), channel_id=1, source_target_pairs={{0,1},{1,2},{2,3},{3,0},{4,5},{5,6},{6,7},{7,4},{8,9},{9,10},{10,1... | collective-permute-start | bytes 1179656 | tf_op jit(solution)/shard_map/ppermute | solution.py:17
  269.7 18.9 %collective-permute-start.4 = (bf16[256,768]{1,0:T(8,128)(2,1)S(1)}, bf16[256,768]{1,0:T(8,128)(2,1)S(1)}, u32[]{:S(2)}, u32[]{:S(2)}) collective-permute-start(bf16[256,768]{1,0:T(8,128)(2,1)S(1)} %get-tuple-element.314), channel_id=1, source_target_pairs={{0,3},{1,0},{2,1},{3,2},{4,7},{5,4},{6,5},{7,6},{8,11},{9,8},{10,9... | collective-permute-start | bytes 1179656 | tf_op jit(solution)/shard_map/ppermute | solution.py:20
  283.4 15.4 %collective-permute-start.5 = (bf16[256,768]{1,0:T(8,128)(2,1)S(1)}, bf16[256,768]{1,0:T(8,128)(2,1)S(1)}, u32[]{:S(2)}, u32[]{:S(2)}) collective-permute-start(bf16[256,768]{1,0:T(8,128)(2,1)S(1)} %collective-permute-done.3), channel_id=1, source_target_pairs={{0,1},{1,2},{2,3},{3,0},{4,5},{5,6},{6,7},{7,4},{8,9},{9,10},{10,1... | collective-permute-start | bytes 1179656 | tf_op jit(solution)/shard_map/ppermute | solution.py:17
  301.6 2.3 copy-start.6
  312.2 2.3 copy-start.6
  329.2 3.7 copy-start.5
  329.2 3.7 copy-start.17
  329.2 162.5 %all-reduce.8.cloned.1.call-start = ((), (), s32[]{:S(2)}) async-start(), calls=%async_computation.11 | async-start | bytes 7077888 | tf_op jit(solution)/shard_map/psum | solution.py:295
  332.9 4.1 copy-start.36
  334.2 2.8 copy-start.20
  339.3 23.7 %copy-start.2 = (f32[256,768]{1,0:T(8,128)S(1)}, f32[256,768]{1,0:T(8,128)}, u32[]{:S(2)}) copy-start(f32[256,768]{1,0:T(8,128)} %copy-done.1) | copy-start | bytes 2359300
  339.3 25.1 %copy-start.4 = (f32[256,768]{1,0:T(8,128)S(1)}, f32[256,768]{1,0:T(8,128)}, u32[]{:S(2)}) copy-start(f32[256,768]{1,0:T(8,128)} %copy-done.3) | copy-start | bytes 2359300
  339.3 240.0 %all-reduce.6.cloned.1.call-start = ((), (), s32[]{:S(2)}) async-start(), calls=%async_computation.10 | async-start | bytes 3145728 | tf_op jit(solution)/shard_map/psum | solution.py:315
  364.4 1.3 copy-start.29
  365.7 2.3 copy-start.9
  368.0 58.5 %copy-start.8 = (bf16[2,512,3,192]{1,3,2,0:T(8,128)(2,1)S(1)}, bf16[2,512,3,192]{1,3,2,0:T(8,128)(2,1)}, u32[]{:S(2)}) copy-start(bf16[2,512,3,192]{1,3,2,0:T(8,128)(2,1)} %get-tuple-element.159) | copy-start | bytes 3538948
  579.3 2.9 copy-start.23
  579.3 3.7 copy-start.22
  582.2 1.6 copy-start.21
  582.2 2.5 copy-start.14
  (6 other events, 6.8 us)
Sparse Core Ops, SparseCore 0:
  10.4 39.8 all-gather.2
  90.0 38.1 reduce-scatter.4
  130.8 54.2 all-gather.4
  193.7 34.8 reduce-scatter.8
  230.7 34.2 reduce-scatter.6
  329.3 33.5 reduce-scatter.10
  367.8 72.8 all-reduce.7
  446.5 132.7 all-reduce.5
